TPU v7x, 32 devices: a whole 2x2x4 slice. The times are simulated.
32 devices in a mesh: expert: 8 (over z, y), tensor: 4 (over x, core).
Axes of the slice: x: 2, y: 2, z: 4, core: 2. Of those that a mesh axis runs over, the one named last changes fastest.
Arguments:
- tokens: bfloat16 [1024, 3072], P('expert', 'tensor'), may hold values from -6 to 6
- expert_ids: int32 [1024, 2], P('expert'), may hold values from 0 to 7, all different within a row; in each aligned block of 128 rows (0 to 127, 128 to 255, ...) at most 48 rows name the same one
- joined_weight: bfloat16 [8, 3072, 2, 16384], P('expert', 'tensor'), may hold values from -0.109375 to 0.109375
Outputs:
- hidden: bfloat16 [1024, 2, 1, 16384], P('expert', None, None, 'tensor')
Inputs may be any that keep to these rules, and one draw needn't show every extreme that they name: `expert_ids`: each row names 2 different experts. Among the rows of one device (each aligned block of 128 rows) no expert is named by more than 48 rows, and in some blocks one expert is named by exactly 48 rows.
All inputs are finite; a program needn't handle non-finite values.
Results may differ from a plain program's by a relative error of at most 0.001.
Values may be sent and summed in bfloat16 or wider, within the bound.
A program may use at most 256 MiB of HBM per device.

v0:
```python
import jax
import jax.numpy as jnp
from jax import lax
from jax.sharding import PartitionSpec as P

E = 8
TOP = 2
CAP = 48


def activate(gate_up, half_width):
    gate = gate_up[:, :half_width]
    upward = gate_up[:, half_width:]
    return (jax.nn.silu(gate) * upward).astype(jnp.bfloat16)


def give_back(active):
    return lax.all_to_all(active, "expert", split_axis=0, concat_axis=0, tiled=True)


def local(tokens, expert_ids, joined_weight):
    groups = lax.axis_size("tensor")
    blocks = lax.axis_size("expert")
    copies = blocks // E
    local_rows = joined_weight.shape[1]
    half_width = joined_weight.shape[3] // groups
    pieces = joined_weight[0].reshape(local_rows, 2, groups, half_width)
    arranged = lax.all_to_all(pieces, "tensor", split_axis=2, concat_axis=0, tiled=True)
    weights = arranged.reshape(local_rows * groups, 2 * half_width)
    tok_count = tokens.shape[0]
    flat_ids = expert_ids.reshape(-1)
    chosen = (flat_ids[:, None] == jnp.arange(E, dtype=jnp.int32)[None, :]).astype(jnp.int32)
    earlier = jnp.cumsum(chosen, axis=0) - chosen
    position = jnp.sum(earlier * chosen, axis=1)
    slot_index = flat_ids * CAP + position
    pick_table = (slot_index[:, None] == jnp.arange(E * CAP, dtype=jnp.int32)[None, :]).astype(
        jnp.bfloat16
    )
    token_table = pick_table.reshape(tok_count, TOP, E * CAP).sum(axis=1)
    complete = lax.all_gather(tokens, "tensor", axis=1, tiled=True)
    width = complete.shape[1]
    placed = lax.dot_general(
        token_table, complete, (((0,), (0,)), ((), ())), preferred_element_type=jnp.float32
    )
    placed = placed.astype(jnp.bfloat16).reshape(E, 1, CAP, width)
    outgoing = jnp.broadcast_to(placed, (E, copies, CAP, width)).reshape(blocks, CAP, width)
    received = lax.all_to_all(outgoing, "expert", split_axis=0, concat_axis=0, tiled=True)
    slot_count = received.shape[1]
    row_block = received.reshape(blocks * slot_count, received.shape[2])
    gate_up = jnp.dot(row_block, weights, preferred_element_type=jnp.float32)
    returned = give_back(activate(gate_up, half_width).reshape(blocks, slot_count, half_width))
    grouped = (
        returned.reshape(E, copies, CAP, half_width)
        .transpose(0, 2, 1, 3)
        .reshape(E * CAP, copies * half_width)
    )
    hidden = jnp.dot(pick_table, grouped, preferred_element_type=jnp.float32).astype(jnp.bfloat16)
    return hidden.reshape(tok_count, TOP, copies, half_width)


def solution(mesh):
    placed = (P("expert", "tensor"), P("expert", None), P("expert", "tensor", None, None))
    return jax.shard_map(
        local,
        mesh=mesh,
        in_specs=placed,
        out_specs=P("expert", None, None, "tensor"),
        check_vma=False,
    )
```

profile of v0, /device:TPU:0, one launch (start us, length us, event | category | flops | bytes accessed | tf_op | source)
XLA Modules:
  0.0 907.6 jit_solution(4300740017279829899)
XLA Ops:
  0.0 78.4 %reshape_squeeze.3 = bf16[768,2,4,4096]{3,2,1,0:T(4,128)(2,1)} reshape(bf16[1,768,2,16384]{3,2,1,0:T(2,128)(2,1)} %param.5) | data formatting | bytes 100663296 | tf_op jit(solution)/shard_map/reshape;squeeze | solution.py:27
  78.4 88.9 %copy.22 = bf16[768,2,4,4096]{3,1,0,2:T(2,128)(2,1)} copy(bf16[768,2,4,4096]{3,2,1,0:T(4,128)(2,1)} %reshape_squeeze.3) | data formatting | bytes 100663296 | tf_op jit(solution)/shard_map/reshape;squeeze | solution.py:27
  167.3 0.0 copy-start.1
  167.3 0.0 copy-start
  167.3 12.0 %all-to-all-start.1 = ((bf16[768,2,4,4096]{3,1,0,2:T(2,128)(2,1)}), bf16[768,2,4,4096]{3,1,0,2:T(2,128)(2,1)}, u32[]{:S(2)}, u32[]{:S(2)}) async-start(bf16[768,2,4,4096]{3,1,0,2:T(2,128)(2,1)} %copy.22), calls=%async_computation.1 | async-start | bytes 100663296 | tf_op jit(solution)/shard_map/all_to_all | solution.py:28
  179.3 0.0 copy-done.1
  179.3 0.1 copy.19
  179.5 0.1 reshape.51
  179.6 0.1 eq.46
  179.8 0.6 reduce-window.6
  180.3 0.2 slice_reduce_fusion
  180.6 0.1 fusion.5
  180.7 0.1 reduce_sum.24
  180.8 0.1 copy.21
  180.9 0.1 fusion.2
  181.0 0.0 copy-done
  181.1 546.4 %all_gather.3 = bf16[128,3072]{1,0:T(8,128)(2,1)S(1)} all-gather(bf16[128,768]{1,0:T(8,128)(2,1)S(1)} %copy-done), channel_id=1, replica_groups=mesh['expert'=8,'tensor'=4] {'tensor'}, dimensions={1}, use_global_device_ids=true | all-gather | bytes 983040 | tf_op jit(solution)/shard_map/all_gather | solution.py:40
  727.4 2.2 convolution_convert_fusion.1
  729.6 0.0 all-to-all-done.1
  729.6 6.8 all-to-all-start
  736.4 42.8 %copy.24 = bf16[384,8,2,4096]{3,1,2,0:T(8,128)(2,1)} copy(bf16[384,8,2,4096]{3,2,1,0:T(2,128)(2,1)} %bitcast.13) | data formatting | bytes 100663296
  779.2 11.6 %all-to-all-done = bf16[8,48,3072]{2,1,0:T(8,128)(2,1)S(1)} async-done(((bf16[8,48,3072]{2,1,0:T(8,128)(2,1)}), bf16[8,48,3072]{2,1,0:T(8,128)(2,1)S(1)}, u32[]{:S(2)}, u32[]{:S(2)}) %all-to-all-start) | async-done | bytes 2359328 | tf_op jit(solution)/shard_map/all_to_all | solution.py:47
  790.8 28.6 %fusion.7 = f32[384,8192]{1,0:T(8,128)} fusion(bf16[384,3072]{1,0:T(8,128)(2,1)S(1)} %bitcast.28, bf16[3072,8192]{1,0:T(8,128)(2,1)} %bitcast.25), kind=kOutput, calls=%fused_computation.18 | convolution fusion | flops 19327352832 | bytes 65273856 | tf_op jit(solution)/shard_map/dot_general | solution.py:50
  819.4 6.7 fusion
  826.1 3.6 all-to-all-start.2
  829.7 70.9 %all-to-all-done.2 = bf16[8,48,4096]{2,1,0:T(8,128)(2,1)S(1)} async-done(((bf16[8,48,4096]{2,1,0:T(8,128)(2,1)}), bf16[8,48,4096]{2,1,0:T(8,128)(2,1)S(1)}, u32[]{:S(2)}, u32[]{:S(2)}) %all-to-all-start.2) | async-done | bytes 3145760 | tf_op jit(solution)/shard_map/all_to_all | solution.py:18
  900.6 2.6 convolution_convert_fusion
  903.2 4.4 reshape.56
  (5 shorter events, 0.1 us)
Async XLA Ops:
  167.3 12.0 %copy-start.1 = (s32[128,2]{0,1:T(2,128)S(1)}, s32[128,2]{0,1:T(2,128)}, u32[]{:S(2)}) copy-start(s32[128,2]{0,1:T(2,128)} %param.4) | copy-start | bytes 3076
  167.3 13.7 %copy-start = (bf16[128,768]{1,0:T(8,128)(2,1)S(1)}, bf16[128,768]{1,0:T(8,128)(2,1)}, u32[]{:S(2)}) copy-start(bf16[128,768]{1,0:T(8,128)(2,1)} %param.3) | copy-start | bytes 589828
  167.3 562.3 %all-to-all-start.1 = ((bf16[768,2,4,4096]{3,1,0,2:T(2,128)(2,1)}), bf16[768,2,4,4096]{3,1,0,2:T(2,128)(2,1)}, u32[]{:S(2)}, u32[]{:S(2)}) async-start(bf16[768,2,4,4096]{3,1,0,2:T(2,128)(2,1)} %copy.22), calls=%async_computation.1 | async-start | bytes 100663296 | tf_op jit(solution)/shard_map/all_to_all | solution.py:28
  729.6 61.1 %all-to-all-start = ((bf16[8,48,3072]{2,1,0:T(8,128)(2,1)}), bf16[8,48,3072]{2,1,0:T(8,128)(2,1)S(1)}, u32[]{:S(2)}, u32[]{:S(2)}) async-start(bf16[8,48,3072]{2,1,0:T(8,128)(2,1)} %bitcast.2), calls=%async_computation | async-start | bytes 4718592 | tf_op jit(solution)/shard_map/all_to_all | solution.py:47
  826.1 74.5 %all-to-all-start.2 = ((bf16[8,48,4096]{2,1,0:T(8,128)(2,1)}), bf16[8,48,4096]{2,1,0:T(8,128)(2,1)S(1)}, u32[]{:S(2)}, u32[]{:S(2)}) async-start(bf16[8,48,4096]{2,1,0:T(8,128)(2,1)} %bitcast.27), calls=%async_computation.2 | async-start | bytes 6291456 | tf_op jit(solution)/shard_map/all_to_all | solution.py:18
where the time goes:
time: 910 us; the launch traced here: 908 us
  blocking collectives  546 us (60%)
  local copies, waits for them, and re-layouts  215 us (24%)
  waiting for transfers between devices  82.4 us (9%)
  matrix products  33.5 us (4%)
  starting transfers between devices  22.4 us (2%)
    all_gather x1, blocking collectives, local(): complete = lax.all_gather(tokens, 'tensor', axis=1, tiled=True)  546 us
    another operation x2, local copies, waits for them, and re-layouts, local(): pieces = joined_weight[0].reshape(local_rows, 2, groups, half_width)  167 us
    all_to_all x1, waiting for transfers between devices, give_back(): lax.all_to_all(active, 'expert', split_axis=0, concat_axis=0, tiled=True)  70.9 us
    unnamed x6, local copies, waits for them, and re-layouts  42.9 us
    dot_general x1, matrix products, local(): gate_up = jnp.dot(row_block, weights, preferred_element_type=jnp.float32)  28.6 us
  transfers between devices with their start and end apart: 3, of which 2 were waited for; matrix products, arithmetic and copies ran while one was open for 5% of the time, Pallas kernels for 0%

commit v1 on v0

--- a/solution.py
+++ b/solution.py
@@ -37,7 +37,7 @@
         jnp.bfloat16
     )
     token_table = pick_table.reshape(tok_count, TOP, E * CAP).sum(axis=1)
-    complete = lax.all_gather(tokens, "tensor", axis=1, tiled=True)
+    complete = jnp.concatenate(lax.all_gather(tokens, "tensor"), axis=1)
     width = complete.shape[1]
     placed = lax.dot_general(
         token_table, complete, (((0,), (0,)), ((), ())), preferred_element_type=jnp.float32

time: 910 us -> 911 us (level)
  no operation moved by 1% of the time
where the time goes in v1:
time: 911 us; the launch traced here: 908 us
  blocking collectives  547 us (60%)
  local copies, waits for them, and re-layouts  216 us (24%)
  waiting for transfers between devices  82.4 us (9%)
  matrix products  33.5 us (4%)
  starting transfers between devices  22.4 us (2%)
    all_gather x1, blocking collectives, local(): complete = jnp.concatenate(lax.all_gather(tokens, 'tensor'), axis=1)  547 us
    another operation x2, local copies, waits for them, and re-layouts, local(): pieces = joined_weight[0].reshape(local_rows, 2, groups, half_width)  167 us
    all_to_all x1, waiting for transfers between devices, give_back(): lax.all_to_all(active, 'expert', split_axis=0, concat_axis=0, tiled=True)  70.9 us
    unnamed x6, local copies, waits for them, and re-layouts  42.9 us
    dot_general x1, matrix products, local(): gate_up = jnp.dot(row_block, weights, preferred_element_type=jnp.float32)  28.6 us
  transfers between devices with their start and end apart: 3, of which 2 were waited for; matrix products, arithmetic and copies ran while one was open for 5% of the time, Pallas kernels for 0%

profile of v1, /device:TPU:0, one launch (start us, length us, event | category | flops | bytes accessed | tf_op | source)
XLA Modules:
  0.0 908.1 jit_solution(4278358120468542115)
XLA Ops:
  0.0 78.4 %reshape_squeeze.3 = bf16[768,2,4,4096]{3,2,1,0:T(4,128)(2,1)} reshape(bf16[1,768,2,16384]{3,2,1,0:T(2,128)(2,1)} %param.5) | data formatting | bytes 100663296 | tf_op jit(solution)/shard_map/reshape;squeeze | solution.py:27
  78.4 88.9 %copy.31 = bf16[768,2,4,4096]{3,1,0,2:T(2,128)(2,1)} copy(bf16[768,2,4,4096]{3,2,1,0:T(4,128)(2,1)} %reshape_squeeze.3) | data formatting | bytes 100663296 | tf_op jit(solution)/shard_map/reshape;squeeze | solution.py:27
  167.3 0.0 copy-start.1
  167.3 0.0 copy-start
  167.3 12.0 %all-to-all-start.1 = ((bf16[768,2,4,4096]{3,1,0,2:T(2,128)(2,1)}), bf16[768,2,4,4096]{3,1,0,2:T(2,128)(2,1)}, u32[]{:S(2)}, u32[]{:S(2)}) async-start(bf16[768,2,4,4096]{3,1,0,2:T(2,128)(2,1)} %copy.31), calls=%async_computation.1 | async-start | bytes 100663296 | tf_op jit(solution)/shard_map/all_to_all | solution.py:28
  179.3 0.0 copy-done.1
  179.3 0.1 copy.27
  179.5 0.1 reshape.57
  179.6 0.1 eq.46
  179.8 0.6 reduce-window.6
  180.3 0.2 slice_reduce_fusion
  180.6 0.1 fusion.5
  180.7 0.1 reduce_sum.24
  180.8 0.1 copy.29
  180.9 0.0 copy-done
  180.9 546.5 %all-gather = bf16[512,768]{1,0:T(8,128)(2,1)S(1)} all-gather(bf16[128,768]{1,0:T(8,128)(2,1)S(1)} %copy-done), channel_id=2, replica_groups=mesh['expert'=8,'tensor'=4] {'tensor'}, dimensions={0}, use_global_device_ids=true | all-gather | bytes 983040 | tf_op jit(solution)/shard_map/all_gather | solution.py:40
  727.4 0.4 copy.30
  727.8 0.1 fusion.2
  727.9 2.2 convolution_convert_fusion.1
  730.1 0.0 all-to-all-done.1
  730.1 6.8 all-to-all-start
  736.9 42.8 %copy.33 = bf16[384,8,2,4096]{3,1,2,0:T(8,128)(2,1)} copy(bf16[384,8,2,4096]{3,2,1,0:T(2,128)(2,1)} %bitcast.17) | data formatting | bytes 100663296
  779.7 11.6 %all-to-all-done = bf16[8,48,3072]{2,1,0:T(8,128)(2,1)S(1)} async-done(((bf16[8,48,3072]{2,1,0:T(8,128)(2,1)}), bf16[8,48,3072]{2,1,0:T(8,128)(2,1)S(1)}, u32[]{:S(2)}, u32[]{:S(2)}) %all-to-all-start) | async-done | bytes 2359328 | tf_op jit(solution)/shard_map/all_to_all | solution.py:47
  791.3 28.6 %fusion.7 = f32[384,8192]{1,0:T(8,128)} fusion(bf16[384,3072]{1,0:T(8,128)(2,1)S(1)} %bitcast.34, bf16[3072,8192]{1,0:T(8,128)(2,1)} %bitcast.29), kind=kOutput, calls=%fused_computation.18 | convolution fusion | flops 19327352832 | bytes 65273856 | tf_op jit(solution)/shard_map/dot_general | solution.py:50
  819.9 6.7 fusion
  826.6 3.6 all-to-all-start.2
  830.2 70.9 %all-to-all-done.2 = bf16[8,48,4096]{2,1,0:T(8,128)(2,1)S(1)} async-done(((bf16[8,48,4096]{2,1,0:T(8,128)(2,1)}), bf16[8,48,4096]{2,1,0:T(8,128)(2,1)S(1)}, u32[]{:S(2)}, u32[]{:S(2)}) %all-to-all-start.2) | async-done | bytes 3145760 | tf_op jit(solution)/shard_map/all_to_all | solution.py:18
  901.1 2.7 convolution_convert_fusion
  903.8 4.4 reshape.64
  (5 shorter events, 0.1 us)
Async XLA Ops:
  167.3 12.0 %copy-start.1 = (s32[128,2]{0,1:T(2,128)S(1)}, s32[128,2]{0,1:T(2,128)}, u32[]{:S(2)}) copy-start(s32[128,2]{0,1:T(2,128)} %param.4) | copy-start | bytes 3076
  167.3 13.6 %copy-start = (bf16[128,768]{1,0:T(8,128)(2,1)S(1)}, bf16[128,768]{1,0:T(8,128)(2,1)}, u32[]{:S(2)}) copy-start(bf16[128,768]{1,0:T(8,128)(2,1)} %param.3) | copy-start | bytes 589828
  167.3 562.8 %all-to-all-start.1 = ((bf16[768,2,4,4096]{3,1,0,2:T(2,128)(2,1)}), bf16[768,2,4,4096]{3,1,0,2:T(2,128)(2,1)}, u32[]{:S(2)}, u32[]{:S(2)}) async-start(bf16[768,2,4,4096]{3,1,0,2:T(2,128)(2,1)} %copy.31), calls=%async_computation.1 | async-start | bytes 100663296 | tf_op jit(solution)/shard_map/all_to_all | solution.py:28
  730.1 61.1 %all-to-all-start = ((bf16[8,48,3072]{2,1,0:T(8,128)(2,1)}), bf16[8,48,3072]{2,1,0:T(8,128)(2,1)S(1)}, u32[]{:S(2)}, u32[]{:S(2)}) async-start(bf16[8,48,3072]{2,1,0:T(8,128)(2,1)} %bitcast.5), calls=%async_computation | async-start | bytes 4718592 | tf_op jit(solution)/shard_map/all_to_all | solution.py:47
  826.6 74.5 %all-to-all-start.2 = ((bf16[8,48,4096]{2,1,0:T(8,128)(2,1)}), bf16[8,48,4096]{2,1,0:T(8,128)(2,1)S(1)}, u32[]{:S(2)}, u32[]{:S(2)}) async-start(bf16[8,48,4096]{2,1,0:T(8,128)(2,1)} %bitcast.31), calls=%async_computation.2 | async-start | bytes 6291456 | tf_op jit(solution)/shard_map/all_to_all | solution.py:18
